TPU v7x, 32 devices: a whole 2x2x4 slice. The times are simulated.
32 devices in a mesh: group: 8 (over z, core), helper: 4 (over y, x).
Axes of the slice: x: 2, y: 2, z: 4, core: 2. Of those that a mesh axis runs over, the one named last changes fastest.
Arguments:
- candidates: bfloat16 [64, 128, 1024], P(('group', 'helper')), may hold values from -36 to 36
- block_user: int32 [64], P(('group', 'helper')), may hold values from 0 to 3, as said below
- live_rows: int32 [64], P(('group', 'helper')), may hold values from 1 to 128
- prefix_keys: bfloat16 [32, 256, 1024], P(('group', 'helper')), may hold values from -6 to 6
- prefix_values: bfloat16 [32, 256, 1024], P(('group', 'helper')), may hold values from -6 to 6
- w_proj: bfloat16 [1024, 4096], P(('group', 'helper')), may hold values from -0.1875 to 0.1875
- w_out: bfloat16 [1024, 1024], P(('group', 'helper')), may hold values from -0.1875 to 0.1875
- gain_in: float32 [1024], replicated, may hold values from 0.1 to 1.9
- gain_mid: float32 [1024], replicated, may hold values from 0.1 to 1.9
- score_vec: float32 [1024], replicated, may hold values from -0.1875 to 0.1875
Outputs:
- embeddings: bfloat16 [64, 128, 1024], P(('group', 'helper'))
- scores: float32 [64, 128], P(('group', 'helper'))
Inputs may be any that keep to these rules, and one draw needn't show every extreme that they name: `block_user`: the 2 blocks of one device name different users; in every group some user is named by a block of every device of the group.
All inputs are finite; a program needn't handle non-finite values.
Results may differ from a plain program's by a relative error of at most 0.0045.
Values may be sent and summed in bfloat16 or wider, within the bound.
No kernel may reach another device: no remote copies, remote signals or barrier semaphores. Data moves between devices by JAX's collectives and lax.ppermute only.
A program may use at most 128 MiB of HBM per device.

v0:
```python
import jax
import jax.numpy as jnp
from jax import lax
from jax.sharding import PartitionSpec as P

HEADS = 8
epsilon = 1e-05


def layer_norm(values, gain):
    average = jnp.mean(values, axis=-1, keepdims=True)
    centred = values - average
    spread = jnp.mean(centred * centred, axis=-1, keepdims=True)
    return centred * lax.rsqrt(spread + epsilon) * gain


def shards(
    candidates,
    block_user,
    live_rows,
    prefix_keys,
    prefix_values,
    w_proj,
    w_out,
    gain_in,
    gain_mid,
    score_vec,
):
    helpers = lax.axis_size("helper")
    blocks, rows_block, features = candidates.shape
    head_dim = features // HEADS
    score_scale = head_dim ** (-0.5)
    proj_full, out_full = (
        lax.all_gather(w_proj, ("group", "helper"), axis=0, tiled=True),
        lax.all_gather(w_out, ("group", "helper"), axis=0, tiled=True),
    )
    cand_rows = candidates.reshape(blocks * rows_block, features).astype(jnp.float32)
    normed = layer_norm(cand_rows, gain_in).astype(jnp.bfloat16)
    projected = jax.nn.silu(jnp.dot(normed, proj_full, preferred_element_type=jnp.float32))
    gate_portion = projected[:, :features]
    value_part = projected[:, features : 2 * features]
    query_portion = projected[:, 2 * features : 3 * features]
    key_part = projected[:, 3 * features :]
    query_bf = lax.optimization_barrier(query_portion.astype(jnp.bfloat16))
    query_heads = query_bf.astype(jnp.float32).reshape(-1, HEADS, head_dim)
    own_weight = jax.nn.silu(
        score_scale * jnp.sum(query_heads * key_part.reshape(-1, HEADS, head_dim), axis=-1)
    )
    own_term = (own_weight[..., None] * value_part.reshape(-1, HEADS, head_dim)).reshape(
        -1, features
    )
    onehot = (block_user[None, :] == jnp.arange(helpers, dtype=jnp.int32)[:, None]).astype(
        jnp.bfloat16
    )
    outgoing = jnp.dot(
        onehot, query_bf.reshape(blocks, rows_block * features), preferred_element_type=jnp.float32
    )
    outgoing = outgoing.astype(jnp.bfloat16).reshape(helpers, rows_block, features)
    per_head_keys = prefix_keys[0].reshape(-1, HEADS, head_dim)
    per_head_values = prefix_values[0].reshape(-1, HEADS, head_dim)

    def attended_row_set(query_tile_group):
        raw_scores = jnp.einsum(
            "ocy,qcy->coq", query_tile_group, per_head_keys, preferred_element_type=jnp.float32
        )
        weight_brainfloat = jax.nn.silu(score_scale * raw_scores).astype(jnp.bfloat16)
        return jnp.einsum(
            "txw,wta->xta", weight_brainfloat, per_head_values, preferred_element_type=jnp.float32
        ).astype(jnp.bfloat16)

    arrived = lax.all_to_all(outgoing, "helper", split_axis=0, concat_axis=0, tiled=True)
    arrived_shape = arrived.shape
    count_rows = arrived_shape[0] * arrived_shape[1]
    flat_query = arrived.reshape(count_rows, HEADS, head_dim)
    if count_rows > 512 and count_rows % 512 == 0:
        mixed_heads = lax.map(
            attended_row_set, flat_query.reshape(count_rows // 512, 512, HEADS, head_dim)
        )
    else:
        mixed_heads = attended_row_set(flat_query)
    returned = lax.all_to_all(
        mixed_heads.reshape(arrived_shape), "helper", split_axis=0, concat_axis=0, tiled=True
    )
    prefix_mix = jnp.einsum(
        "jb,jf->bf",
        onehot,
        returned.reshape(helpers, rows_block * features),
        preferred_element_type=jnp.float32,
    )
    mixed = prefix_mix.reshape(-1, features) + own_term
    gated = (layer_norm(mixed, gain_mid) * gate_portion).astype(jnp.bfloat16)
    updated = cand_rows + jnp.dot(gated, out_full, preferred_element_type=jnp.float32)
    embeddings = updated.astype(jnp.bfloat16).reshape(blocks, rows_block, features)
    row_scores = jnp.sum(layer_norm(updated, 1.0) * score_vec, axis=-1).reshape(blocks, rows_block)
    live_mask = jnp.arange(rows_block, dtype=jnp.int32)[None, :] < live_rows[:, None]
    scores = jnp.where(live_mask, row_scores, jnp.zeros_like(row_scores))
    return (embeddings, scores)


def solution(mesh):
    placed = (
        P(("group", "helper"), None, None),
        P(("group", "helper")),
        P(("group", "helper")),
        P(("group", "helper"), None, None),
        P(("group", "helper"), None, None),
        P(("group", "helper"), None),
        P(("group", "helper"), None),
        P(),
        P(),
        P(),
    )
    return jax.shard_map(
        shards,
        mesh=mesh,
        in_specs=placed,
        out_specs=(P(("group", "helper"), None, None), P(("group", "helper"), None)),
        check_vma=False,
    )
```

profile of v0, /device:TPU:0, one launch (start us, length us, event | category | flops | bytes accessed | tf_op | source)
XLA Modules:
  0.0 164.2 jit_solution(251757091519188598)
XLA Ops:
  7.2 0.0 all-gather.3.cloned.1.call-start
  7.2 0.7 all-gather.3.cloned.1.call-update
  7.9 0.0 all-gather.5.cloned.1.call-start
  7.9 0.7 all-gather.5.cloned.1.call-update
  8.6 1.2 convert_reduce_fusion
  9.8 1.3 multiply_reduce_fusion.3
  11.2 1.3 fusion.8
  12.5 0.0 copy-start.6
  12.5 78.1 %all-gather.3.cloned.1.call-done = bf16[1024,4096]{1,0:T(8,128)(2,1)} async-done(((bf16[32,4096]{1,0:T(8,128)(2,1)}), bf16[1024,4096]{1,0:T(8,128)(2,1)}) %all-gather.3.cloned.1.call-update) | async-done | bytes 8388624 | tf_op jit(solution)/shard_map/all_gather | solution.py:34
  90.7 5.9 %divide_multiply_fusion = f32[256,4096]{1,0:T(8,128)S(1)} fusion(bf16[256,1024]{1,0:T(8,128)(2,1)S(1)} %fusion.8, bf16[1024,4096]{1,0:T(8,128)(2,1)} %all-gather.3.cloned.1.call-done), kind=kOutput, calls=%fused_computation.2 | convolution fusion | flops 2151677952 | bytes 13107200 | tf_op jit(solution)/shard_map/dot_general | solution.py:39
  96.5 0.0 copy-start.1
  96.5 1.9 %copy-done.1 = f32[256,4096]{1,0:T(8,128)} copy-done((f32[256,4096]{1,0:T(8,128)}, f32[256,4096]{1,0:T(8,128)S(1)}, u32[]{:S(2)}) %copy-start.1) | copy-done | bytes 4194328
  98.5 0.1 slice.30
  98.5 0.4 reshape.106
  98.9 0.0 copy-start.2
  98.9 0.0 copy-start.3
  99.0 0.7 convolution_convert_fusion
  99.7 1.3 copy.47
  100.9 3.5 %all-to-all-start = ((bf16[4,128,1024]{2,1,0:T(8,128)(2,1)}), bf16[4,128,1024]{2,1,0:T(8,128)(2,1)S(1)}, u32[]{:S(2)}, u32[]{:S(2)}) async-start(bf16[4,128,1024]{2,1,0:T(8,128)(2,1)} %bitcast.46), calls=%async_computation | async-start | bytes 2097152 | tf_op jit(solution)/shard_map/all_to_all | solution.py:71
  104.5 0.1 copy.31
  104.6 0.0 copy-done.3
  104.6 0.9 copy.32
  105.5 13.3 %all-to-all-done = bf16[4,128,1024]{2,1,0:T(8,128)(2,1)S(1)} async-done(((bf16[4,128,1024]{2,1,0:T(8,128)(2,1)}), bf16[4,128,1024]{2,1,0:T(8,128)(2,1)S(1)}, u32[]{:S(2)}, u32[]{:S(2)}) %all-to-all-start) | async-done | bytes 1048608 | tf_op jit(solution)/shard_map/all_to_all | solution.py:71
  118.8 0.3 copy.30
  119.0 3.8 %fusion.2 = bf16[512,8,128]{2,0,1:T(8,128)(2,1)} fusion(bf16[512,8,128]{2,1,0:T(8,128)(2,1)S(1)} %bitcast.53, bf16[256,8,128]{2,1,0:T(8,128)(2,1)} %bitcast.59, bf16[256,8,128]{2,1,0:T(8,128)(2,1)S(1)} %bitcast.58), kind=kOutput, calls=%fused_computation.5 | convolution fusion | flops 543686656 | bytes 3145728 | tf_op jit(solution)/shard_map/txw,wta->xta/dot_general | solution.py:67
  122.9 1.9 %copy.26 = bf16[512,8,128]{2,1,0:T(8,128)(2,1)S(1)} copy(bf16[512,8,128]{2,0,1:T(8,128)(2,1)} %fusion.2) | data formatting | bytes 2097152 | tf_op jit(solution)/shard_map/convert_element_type | solution.py:69
  124.8 1.3 reshape.109
  126.1 3.7 %all-to-all-start.1 = ((bf16[4,128,1024]{2,1,0:T(8,128)(2,1)}), bf16[4,128,1024]{2,1,0:T(8,128)(2,1)S(1)}, u32[]{:S(2)}, u32[]{:S(2)}) async-start(bf16[4,128,1024]{2,1,0:T(8,128)(2,1)} %reshape.109), calls=%async_computation.1 | async-start | bytes 2097152 | tf_op jit(solution)/shard_map/all_to_all | solution.py:81
  129.8 1.4 fusion.5
  131.2 0.2 copy.34
  131.4 0.3 reduce_sum.74
  131.7 0.1 copy.27
  131.8 0.1 copy.28
  131.9 14.8 %all-to-all-done.1 = bf16[4,128,1024]{2,1,0:T(8,128)(2,1)S(1)} async-done(((bf16[4,128,1024]{2,1,0:T(8,128)(2,1)}), bf16[4,128,1024]{2,1,0:T(8,128)(2,1)S(1)}, u32[]{:S(2)}, u32[]{:S(2)}) %all-to-all-start.1) | async-done | bytes 1048608 | tf_op jit(solution)/shard_map/all_to_all | solution.py:81
  146.7 0.8 copy.33
  147.5 1.1 fusion.18
  148.6 0.0 copy-start
  148.6 0.0 copy-start.4
  148.7 0.9 reshape.111
  149.6 0.3 mul.124
  149.9 1.6 fusion.24
  151.5 0.2 multiply_reduce_fusion.2
  151.8 0.9 all-gather.5.cloned.1.call-done
  152.6 2.8 %fusion.26 = (f32[256]{0:T(256)S(1)}, f32[256,1024]{1,0:T(8,128)S(1)}) fusion(bf16[1024,1024]{1,0:T(8,128)(2,1)} %all-gather.5.cloned.1.call-done, f32[256,4096]{1,0:T(8,128)} %copy-done.1, f32[256,1024]{1,0:T(8,128)S(1)} %get-tuple-element.3, f32[1024]{0:T(1024)S(1)} %copy-done.4, f32[256]{0:T(256)S(1)} %add_rsqrt_fusion.1, ...), kind=kOutput, calls=%fused_computation.46 | convolution fusion | flops 538967808 | bytes 5774336 | tf_op jit(solution)/shard_map/dot_general | solution.py:92
  155.4 0.3 multiply_reduce_fusion.1
  155.7 0.0 copy-done.5
  155.7 1.1 multiply_reduce_fusion
  156.8 0.6 compare_select_fusion
  (14 shorter events, 0.1 us)
Async XLA Ops:
  7.2 83.5 %all-gather.3.cloned.1.call-start = ((), (), s32[]{:S(2)}) async-start(), calls=%async_computation.2 | async-start | bytes 8650752 | tf_op jit(solution)/shard_map/all_gather | solution.py:34
  7.9 144.7 %all-gather.5.cloned.1.call-start = ((), (), s32[]{:S(2)}) async-start(), calls=%async_computation.3 | async-start | bytes 2162688 | tf_op jit(solution)/shard_map/all_gather | solution.py:35
  12.5 86.4 %copy-start.6 = (s32[2]{0:T(128)S(1)}, s32[2]{0:T(128)}, u32[]{:S(2)}) copy-start(s32[2]{0:T(128)} %param.11) | copy-start | bytes 28
  96.5 1.9 %copy-start.1 = (f32[256,4096]{1,0:T(8,128)}, f32[256,4096]{1,0:T(8,128)S(1)}, u32[]{:S(2)}) copy-start(f32[256,4096]{1,0:T(8,128)S(1)} %divide_multiply_fusion) | copy-start | bytes 12582916
  98.9 5.5 %copy-start.2 = (bf16[1,256,1024]{2,1,0:T(8,128)(2,1)S(1)}, bf16[1,256,1024]{2,1,0:T(8,128)(2,1)}, u32[]{:S(2)}) copy-start(bf16[1,256,1024]{2,1,0:T(8,128)(2,1)} %param.13) | copy-start | bytes 1572868
  98.9 5.6 %copy-start.3 = (bf16[1,256,1024]{2,1,0:T(8,128)(2,1)S(1)}, bf16[1,256,1024]{2,1,0:T(8,128)(2,1)}, u32[]{:S(2)}) copy-start(bf16[1,256,1024]{2,1,0:T(8,128)(2,1)} %param.14) | copy-start | bytes 1572868
  100.9 17.8 %all-to-all-start = ((bf16[4,128,1024]{2,1,0:T(8,128)(2,1)}), bf16[4,128,1024]{2,1,0:T(8,128)(2,1)S(1)}, u32[]{:S(2)}, u32[]{:S(2)}) async-start(bf16[4,128,1024]{2,1,0:T(8,128)(2,1)} %bitcast.46), calls=%async_computation | async-start | bytes 2097152 | tf_op jit(solution)/shard_map/all_to_all | solution.py:71
  126.1 20.6 %all-to-all-start.1 = ((bf16[4,128,1024]{2,1,0:T(8,128)(2,1)}), bf16[4,128,1024]{2,1,0:T(8,128)(2,1)S(1)}, u32[]{:S(2)}, u32[]{:S(2)}) async-start(bf16[4,128,1024]{2,1,0:T(8,128)(2,1)} %reshape.109), calls=%async_computation.1 | async-start | bytes 2097152 | tf_op jit(solution)/shard_map/all_to_all | solution.py:81
  148.6 4.0 %copy-start = (bf16[2,128,1024]{2,1,0:T(8,128)(2,1)S(1)}, bf16[2,128,1024]{2,1,0:T(8,128)(2,1)}, u32[]{:S(2)}) copy-start(bf16[2,128,1024]{2,1,0:T(8,128)(2,1)} %param.10) | copy-start | bytes 1572868
  148.6 4.0 %copy-start.4 = (f32[1024]{0:T(1024)S(1)}, f32[1024]{0:T(1024)}, u32[]{:S(2)}) copy-start(f32[1024]{0:T(1024)} %param.18) | copy-start | bytes 12292
  151.5 4.2 %copy-start.5 = (f32[1024]{0:T(1024)S(1)}, f32[1024]{0:T(1024)}, u32[]{:S(2)}) copy-start(f32[1024]{0:T(1024)} %param.19) | copy-start | bytes 12292
  152.6 4.1 %copy-start.7 = (s32[2]{0:T(128)S(1)}, s32[2]{0:T(128)}, u32[]{:S(2)}) copy-start(s32[2]{0:T(128)} %param.12) | copy-start | bytes 28
Sparse Core Ops, SparseCore 0:
  10.8 79.7 all-gather.2
  93.5 59.0 all-gather.4
where the time goes:
time: 165 us; the launch traced here: 164 us
  waiting for transfers between devices  108 us (65%)
  matrix products  14.3 us (9%)
  between operations  14.3 us (9%)
  local copies, waits for them, and re-layouts  10.6 us (6%)
  other arithmetic  9.38 us (6%)
  starting transfers between devices  7.29 us (4%)
    all_gather x1, waiting for transfers between devices, shards(): lax.all_gather(w_proj, ('group', 'helper'), axis=0, tiled=True)  78.1 us
    all_to_all x1, waiting for transfers between devices, shards(): lax.all_to_all(mixed_heads.reshape(arrived_shape), 'helper', split_axis=0...  14.8 us
    all_to_all x1, waiting for transfers between devices, shards(): lax.all_to_all(outgoing, 'helper', split_axis=0, concat_axis=0, tiled=True)  13.3 us
    dot_general x1, matrix products, shards(): jnp.dot(normed, proj_full, preferred_element_type=jnp.float32)  5.86 us
    unnamed x22, local copies, waits for them, and re-layouts  5.51 us
    dot_general x1, matrix products, attended_row_set(): jnp.einsum('txw,wta->xta', weight_brainfloat, per_head_values, preferred_...  3.85 us
    all_to_all x1, starting transfers between devices, shards(): lax.all_to_all(mixed_heads.reshape(arrived_shape), 'helper', split_axis=0...  3.7 us
    all_to_all x1, starting transfers between devices, shards(): lax.all_to_all(outgoing, 'helper', split_axis=0, concat_axis=0, tiled=True)  3.51 us
  transfers between devices with their start and end apart: 4, of which 4 were waited for; matrix products, arithmetic and copies ran while one was open for 17% of the time, Pallas kernels for 0%

commit v1 on v0

--- a/solution.py
+++ b/solution.py
@@ -2,6 +2,7 @@
 import jax.numpy as jnp
 from jax import lax
 from jax.sharding import PartitionSpec as P
+from jax.lax import all_to_all, axis_size
 
 HEADS = 8
 epsilon = 1e-05
@@ -30,8 +31,11 @@
     blocks, rows_block, features = candidates.shape
     head_dim = features // HEADS
     score_scale = head_dim ** (-0.5)
+    quotas_move = lambda local_values, peer_axis, d0: jnp.concatenate(
+        all_to_all(jnp.stack(axis_size(peer_axis) * [local_values]), peer_axis, 0, 0), axis=d0
+    )
     proj_full, out_full = (
-        lax.all_gather(w_proj, ("group", "helper"), axis=0, tiled=True),
+        quotas_move(w_proj, ("group", "helper"), 0),
         lax.all_gather(w_out, ("group", "helper"), axis=0, tiled=True),
     )
     cand_rows = candidates.reshape(blocks * rows_block, features).astype(jnp.float32)

time: 165 us -> 285 us (1.73)
  waiting for transfers between devices: 108 us -> 217 us
  starting transfers between devices: 7.29 us -> 14.7 us
  local copies, waits for them, and re-layouts: 10.6 us -> 16.6 us
  other arithmetic: 9.38 us -> 6.25 us
    all_to_all x0 -> x1, waiting for transfers between devices: none -> 194 us  [shards(): all_to_all(jnp.stack(axis_size(peer_axis) * [local_values]), peer_axis, 0...]
    all_gather x1 -> x0, waiting for transfers between devices: 78.1 us -> none  [shards(): lax.all_gather(w_proj, ('group', 'helper'), axis=0, tiled=True)]
    all_to_all x0 -> x1, starting transfers between devices: none -> 7.45 us  [shards(): all_to_all(jnp.stack(axis_size(peer_axis) * [local_values]), peer_axis, 0...]
    another operation x0 -> x1, local copies, waits for them, and re-layouts: none -> 5.21 us  [shards(): jnp.stack(axis_size(peer_axis) * [local_values])]
    all_to_all x1, waiting for transfers between devices: 14.8 us -> 10.8 us  [shards(): lax.all_to_all(mixed_heads.reshape(arrived_shape), 'helper', split_axis=0...]
    unnamed x22 -> x24, local copies, waits for them, and re-layouts: 5.51 us -> 6.32 us
  transfers between devices with their start and end apart: 4 -> 4, of which waited for: 4 -> 3; matrix products, arithmetic and copies ran while one was open for 17% -> 9% of each run, Pallas kernels for 0% -> 0%
where the time goes in v1:
time: 285 us; the launch traced here: 283 us
  waiting for transfers between devices  217 us (76%)
  local copies, waits for them, and re-layouts  16.6 us (6%)
  starting transfers between devices  14.7 us (5%)
  matrix products  14.4 us (5%)
  between operations  14.3 us (5%)
  other arithmetic  6.25 us (2%)
    all_to_all x1, waiting for transfers between devices, shards(): all_to_all(jnp.stack(axis_size(peer_axis) * [local_values]), peer_axis, 0...  194 us
    all_to_all x1, waiting for transfers between devices, shards(): lax.all_to_all(outgoing, 'helper', split_axis=0, concat_axis=0, tiled=True)  11.8 us
    all_to_all x1, waiting for transfers between devices, shards(): lax.all_to_all(mixed_heads.reshape(arrived_shape), 'helper', split_axis=0...  10.8 us
    all_to_all x1, starting transfers between devices, shards(): all_to_all(jnp.stack(axis_size(peer_axis) * [local_values]), peer_axis, 0...  7.45 us
    unnamed x24, local copies, waits for them, and re-layouts  6.32 us
    dot_general x1, matrix products, shards(): jnp.dot(normed, proj_full, preferred_element_type=jnp.float32)  5.88 us
  transfers between devices with their start and end apart: 4, of which 3 were waited for; matrix products, arithmetic and copies ran while one was open for 9% of the time, Pallas kernels for 0%

profile of v1, /device:TPU:0, one launch (start us, length us, event | category | flops | bytes accessed | tf_op | source)
XLA Modules:
  0.0 283.5 jit_solution(5538355818440011207)
XLA Ops:
  7.2 5.2 %stack.2 = bf16[32,32,4096]{2,1,0:T(8,128)(2,1)} broadcast(bf16[32,4096]{1,0:T(8,128)(2,1)} %param.15), dimensions={1,2} | broadcast | bytes 8650752 | tf_op jit(solution)/shard_map/stack | solution.py:35
  12.4 7.5 %all-to-all-start = ((bf16[32,32,4096]{2,1,0:T(8,128)(2,1)}), bf16[32,32,4096]{2,1,0:T(8,128)(2,1)}, u32[]{:S(2)}, u32[]{:S(2)}) async-start(bf16[32,32,4096]{2,1,0:T(8,128)(2,1)} %stack.2), calls=%async_computation | async-start | bytes 16777216 | tf_op jit(solution)/shard_map/all_to_all | solution.py:35
  19.8 0.0 all-gather.2.cloned.1.call-start
  19.9 0.7 all-gather.2.cloned.1.call-update
  20.6 0.0 copy-done
  20.6 0.1 convert_reduce_fusion
  20.7 0.3 multiply_reduce_fusion.3
  21.0 0.0 copy-done.4
  21.0 0.3 multiply_convert_fusion.1
  21.3 193.9 %all-to-all-done = bf16[32,32,4096]{2,1,0:T(8,128)(2,1)} async-done(((bf16[32,32,4096]{2,1,0:T(8,128)(2,1)}), bf16[32,32,4096]{2,1,0:T(8,128)(2,1)}, u32[]{:S(2)}, u32[]{:S(2)}) %all-to-all-start) | async-done | bytes 8388640 | tf_op jit(solution)/shard_map/all_to_all | solution.py:35
  215.3 5.9 %divide_multiply_fusion = f32[256,4096]{1,0:T(8,128)S(1)} fusion(bf16[256,1024]{1,0:T(8,128)(2,1)S(1)} %bitcast.49, bf16[1024,4096]{1,0:T(8,128)(2,1)} %bitcast.2), kind=kOutput, calls=%fused_computation.2 | convolution fusion | flops 2151677952 | bytes 13107200 | tf_op jit(solution)/shard_map/dot_general | solution.py:43
  221.2 1.9 copy-done.1
  223.1 0.1 slice.30
  223.2 0.4 reshape.119
  223.6 0.0 copy-start.2
  223.6 0.0 copy-start.3
  223.6 0.7 convolution_convert_fusion
  224.3 1.3 copy.47
  225.6 3.5 %all-to-all-start.1 = ((bf16[4,128,1024]{2,1,0:T(8,128)(2,1)}), bf16[4,128,1024]{2,1,0:T(8,128)(2,1)S(1)}, u32[]{:S(2)}, u32[]{:S(2)}) async-start(bf16[4,128,1024]{2,1,0:T(8,128)(2,1)} %bitcast.37), calls=%async_computation.1 | async-start | bytes 2097152 | tf_op jit(solution)/shard_map/all_to_all | solution.py:75
  229.1 0.9 copy.31
  230.0 0.0 copy-done.3
  230.0 0.9 copy.32
  230.9 11.8 %all-to-all-done.1 = bf16[4,128,1024]{2,1,0:T(8,128)(2,1)S(1)} async-done(((bf16[4,128,1024]{2,1,0:T(8,128)(2,1)}), bf16[4,128,1024]{2,1,0:T(8,128)(2,1)S(1)}, u32[]{:S(2)}, u32[]{:S(2)}) %all-to-all-start.1) | async-done | bytes 1048608 | tf_op jit(solution)/shard_map/all_to_all | solution.py:75
  242.7 0.3 copy.30
  243.0 4.0 %fusion.2 = bf16[512,8,128]{2,0,1:T(8,128)(2,1)} fusion(bf16[512,8,128]{2,1,0:T(8,128)(2,1)S(1)} %bitcast.44, bf16[256,8,128]{2,1,0:T(8,128)(2,1)} %bitcast.51, bf16[256,8,128]{2,1,0:T(8,128)(2,1)} %bitcast.50), kind=kOutput, calls=%fused_computation.5 | convolution fusion | flops 543686656 | bytes 3145728 | tf_op jit(solution)/shard_map/txw,wta->xta/dot_general | solution.py:71
  247.0 1.9 copy.26
  248.9 1.3 reshape.122
  250.2 3.7 %all-to-all-start.2 = ((bf16[4,128,1024]{2,1,0:T(8,128)(2,1)}), bf16[4,128,1024]{2,1,0:T(8,128)(2,1)S(1)}, u32[]{:S(2)}, u32[]{:S(2)}) async-start(bf16[4,128,1024]{2,1,0:T(8,128)(2,1)} %reshape.122), calls=%async_computation.2 | async-start | bytes 2097152 | tf_op jit(solution)/shard_map/all_to_all | solution.py:85
  253.9 1.4 fusion.5
  255.2 0.2 copy.34
  255.4 0.3 reduce_sum.74
  255.8 0.1 copy.27
  255.9 0.1 copy.28
  256.0 10.8 %all-to-all-done.2 = bf16[4,128,1024]{2,1,0:T(8,128)(2,1)S(1)} async-done(((bf16[4,128,1024]{2,1,0:T(8,128)(2,1)}), bf16[4,128,1024]{2,1,0:T(8,128)(2,1)S(1)}, u32[]{:S(2)}, u32[]{:S(2)}) %all-to-all-start.2) | async-done | bytes 1048608 | tf_op jit(solution)/shard_map/all_to_all | solution.py:85
  266.8 0.8 copy.33
  267.6 1.1 fusion.15
  268.7 0.0 copy-start.5
  268.7 0.9 reshape.124
  269.6 0.3 mul.126
  270.0 1.6 fusion.20
  271.5 0.2 multiply_reduce_fusion.2
  271.8 0.0 all-gather.2.cloned.1.call-done
  271.9 0.0 copy-start.8
  271.9 2.8 fusion.22
  274.6 0.3 multiply_reduce_fusion.1
  274.9 0.0 copy-done.6
  274.9 1.1 multiply_reduce_fusion
  276.0 0.6 compare_select_fusion
  (16 shorter events, 0.1 us)
Async XLA Ops:
  12.4 8.2 %copy-start = (bf16[2,128,1024]{2,1,0:T(8,128)(2,1)S(1)}, bf16[2,128,1024]{2,1,0:T(8,128)(2,1)}, u32[]{:S(2)}) copy-start(bf16[2,128,1024]{2,1,0:T(8,128)(2,1)} %param.10) | copy-start | bytes 1572868
  12.4 8.7 %copy-start.4 = (f32[1024]{0:T(1024)S(1)}, f32[1024]{0:T(1024)}, u32[]{:S(2)}) copy-start(f32[1024]{0:T(1024)} %param.17) | copy-start | bytes 12292
  12.4 202.9 %all-to-all-start = ((bf16[32,32,4096]{2,1,0:T(8,128)(2,1)}), bf16[32,32,4096]{2,1,0:T(8,128)(2,1)}, u32[]{:S(2)}, u32[]{:S(2)}) async-start(bf16[32,32,4096]{2,1,0:T(8,128)(2,1)} %stack.2), calls=%async_computation | async-start | bytes 16777216 | tf_op jit(solution)/shard_map/all_to_all | solution.py:35
  19.8 252.0 %all-gather.2.cloned.1.call-start = ((), (), s32[]{:S(2)}) async-start(), calls=%async_computation.3 | async-start | bytes 2162688 | tf_op jit(solution)/shard_map/all_gather | solution.py:39
  215.3 8.3 %copy-start.7 = (s32[2]{0:T(128)S(1)}, s32[2]{0:T(128)}, u32[]{:S(2)}) copy-start(s32[2]{0:T(128)} %param.11) | copy-start | bytes 28
  221.2 1.9 copy-start.1
  223.6 5.5 %copy-start.2 = (bf16[1,256,1024]{2,1,0:T(8,128)(2,1)S(1)}, bf16[1,256,1024]{2,1,0:T(8,128)(2,1)}, u32[]{:S(2)}) copy-start(bf16[1,256,1024]{2,1,0:T(8,128)(2,1)} %param.13) | copy-start | bytes 1572868
  223.6 6.4 %copy-start.3 = (bf16[1,256,1024]{2,1,0:T(8,128)(2,1)S(1)}, bf16[1,256,1024]{2,1,0:T(8,128)(2,1)}, u32[]{:S(2)}) copy-start(bf16[1,256,1024]{2,1,0:T(8,128)(2,1)} %param.14) | copy-start | bytes 1572868
  225.6 17.1 %all-to-all-start.1 = ((bf16[4,128,1024]{2,1,0:T(8,128)(2,1)}), bf16[4,128,1024]{2,1,0:T(8,128)(2,1)S(1)}, u32[]{:S(2)}, u32[]{:S(2)}) async-start(bf16[4,128,1024]{2,1,0:T(8,128)(2,1)} %bitcast.37), calls=%async_computation.1 | async-start | bytes 2097152 | tf_op jit(solution)/shard_map/all_to_all | solution.py:75
  250.2 16.6 %all-to-all-start.2 = ((bf16[4,128,1024]{2,1,0:T(8,128)(2,1)}), bf16[4,128,1024]{2,1,0:T(8,128)(2,1)S(1)}, u32[]{:S(2)}, u32[]{:S(2)}) async-start(bf16[4,128,1024]{2,1,0:T(8,128)(2,1)} %reshape.122), calls=%async_computation.2 | async-start | bytes 2097152 | tf_op jit(solution)/shard_map/all_to_all | solution.py:85
  268.7 3.1 %copy-start.5 = (f32[1024]{0:T(1024)S(1)}, f32[1024]{0:T(1024)}, u32[]{:S(2)}) copy-start(f32[1024]{0:T(1024)} %param.18) | copy-start | bytes 12292
  271.5 3.4 %copy-start.6 = (f32[1024]{0:T(1024)S(1)}, f32[1024]{0:T(1024)}, u32[]{:S(2)}) copy-start(f32[1024]{0:T(1024)} %param.19) | copy-start | bytes 12292
  271.9 4.1 %copy-start.8 = (s32[2]{0:T(128)S(1)}, s32[2]{0:T(128)}, u32[]{:S(2)}) copy-start(s32[2]{0:T(128)} %param.12) | copy-start | bytes 28
Sparse Core Ops, SparseCore 0:
  23.5 106.0 all-gather.1
